TPU v7x, 32 devices: a whole 2x2x4 slice. The times are simulated.
32 devices in a mesh: slab: 4 (over y, core), pencil: 8 (over z, x).
Axes of the slice: x: 2, y: 2, z: 4, core: 2. Of those that a mesh axis runs over, the one named last changes fastest.
Arguments:
- density: float32 [128, 768, 512], P('pencil', None, 'slab'), may hold values from -6 to 6
- source: float32 [128, 768, 512], P('pencil', None, 'slab'), may hold values from -6 to 8
- coupling: float32 [3], replicated, may hold values from 0.25 to 2, as said below
- width_inverse: float32 [6, 128, 128], replicated, as said below
- height_inverse: float32 [1, 128, 128], replicated, as said below
- depth_inverse: float32 [4, 128, 128], replicated, as said below
Outputs:
- stepped: float32 [128, 768, 512], P('pencil', None, 'slab')
Inputs may be any that keep to these rules, and one draw needn't show every extreme that they name: coupling holds three positive coefficients. `width_inverse`: block i is the inverse of the i-th pivot block of the block LU factorization of the tridiagonal line matrix with diagonal 1 + 2 s and off-diagonals -s, s the matching coupling. `height_inverse`: as for width_inverse, for the height lines. `depth_inverse`: as for width_inverse, for the depth lines.
All inputs are finite; a program needn't handle non-finite values.
Results may differ from a plain program's by a relative error of at most 0.00027.
Values sent between devices are 32-bit elements; how exact they have to be, the bound alone decides.
A program may use at most 128 MiB of HBM per device.

v0:
```python
import jax
import jax.numpy as jnp
from jax import lax
from jax.sharding import PartitionSpec as P


def extended(value, sides, width):
    for axis, dim in sides:
        count, length = (lax.axis_size(axis), value.shape[dim])
        up = [(i, (i + 1) % count) for i in range(count - 1)]
        down = [(j, i) for i, j in up]
        last = lax.slice_in_dim(value, length - width, length, axis=dim)
        leading = lax.slice_in_dim(value, 0, width, axis=dim)
        before = lax.ppermute(last, axis, up)
        after = lax.ppermute(leading, axis, down)
        value = jnp.concatenate([before, value, after], axis=dim)
    return value


def entering(part, axis, combine, identity, reverse):
    count = lax.axis_size(axis)
    place = lax.axis_index(axis)
    ahead = count - 1 - place if reverse else place
    gathered = jax.tree.map(lambda a: lax.all_gather(a, axis), part)
    state = jax.tree.map(lambda a, e: jnp.zeros_like(a) + jnp.asarray(e, a.dtype), part, identity)

    def one(step, state):
        source = count - 1 - step if reverse else step
        return combine(
            state, jax.tree.map(lambda a: lax.dynamic_index_in_dim(a, source, 0, False), gathered)
        )

    return lax.fori_loop(0, ahead, one, state)


def solve_inner(rhs, inverses, strength):
    outer, length, inner = rhs.shape
    size = inverses.shape[1]
    count = length // size
    blocked = rhs.reshape(outer, count, size, inner)

    def forward(current, state):
        result, carry = state
        piece = lax.dynamic_index_in_dim(blocked, current, 1, keepdims=False)
        matrix = lax.dynamic_index_in_dim(inverses, current, 0, keepdims=False)
        value = jnp.einsum("pkq,jk->pjq", piece, matrix, precision=lax.Precision.HIGHEST)
        value = value + strength * matrix[:, 0][None, :, None] * carry[:, None, :]
        result = lax.dynamic_update_index_in_dim(result, value, current, 1)
        return (result, value[:, size - 1, :])

    start = (jnp.zeros_like(blocked), jnp.zeros((outer, inner), blocked.dtype))
    halfway, unused = lax.fori_loop(0, count, forward, start)

    def backward(step, state):
        result, carry = state
        current = count - 1 - step
        value = lax.dynamic_index_in_dim(result, current, 1, keepdims=False)
        matrix = lax.dynamic_index_in_dim(inverses, current, 0, keepdims=False)
        value = value + strength * matrix[:, size - 1][None, :, None] * carry[:, None, :]
        result = lax.dynamic_update_index_in_dim(result, value, current, 1)
        return (result, value[:, 0, :])

    final, unused = lax.fori_loop(
        0, count, backward, (halfway, jnp.zeros((outer, inner), blocked.dtype))
    )
    return final.reshape(outer, length, inner)


def affine_combine(earlier, later):
    return (later[0] * earlier[0], later[0] * earlier[1] + later[1])


def per_device(density, source, coupling, width_inverse, height_inverse, depth_inverse):
    padded = extended(density, (("slab", 2), ("pencil", 0)), 1)
    center = padded[1:-1, :, 1:-1]
    along_height = padded[2:, :, 1:-1] + padded[:-2, :, 1:-1] - 2.0 * center
    along_depth = padded[1:-1, :, 2:] + padded[1:-1, :, :-2] - 2.0 * center
    width_padded = jnp.pad(density, ((0, 0), (1, 1), (0, 0)))
    along_width = width_padded[:, 2:, :] + width_padded[:, :-2, :] - 2.0 * density
    explicit = (
        2.0 * (coupling[0] * along_width + coupling[1] * along_height + coupling[2] * along_depth)
        + source
    )
    width_step = solve_inner(explicit, width_inverse, coupling[0])
    piece = lax.all_to_all(width_step, "pencil", split_axis=1, concat_axis=0, tiled=True)
    height_step = solve_inner(
        piece.reshape(1, piece.shape[0], -1), height_inverse, coupling[1]
    ).reshape(piece.shape)
    size = depth_inverse.shape[1]
    strength = coupling[2]
    matrix = lax.dynamic_index_in_dim(depth_inverse, lax.axis_index("slab"), 0, keepdims=False)
    local_value = jnp.einsum("yxk,jk->yxj", height_step, matrix, precision=lax.Precision.HIGHEST)
    forward_factor = jnp.reshape(strength * matrix[size - 1, 0], (1, 1))
    unit = jnp.ones((1, 1), local_value.dtype)
    zero_rows = jnp.zeros(local_value.shape[:2], local_value.dtype)
    unused, carry_in = entering(
        (forward_factor, local_value[:, :, size - 1]),
        "slab",
        affine_combine,
        (unit, zero_rows),
        False,
    )
    forward_value = local_value + strength * matrix[:, 0][None, None, :] * carry_in[:, :, None]
    backward_factor = jnp.reshape(strength * matrix[0, size - 1], (1, 1))
    unused, carry_next = entering(
        (backward_factor, forward_value[:, :, 0]), "slab", affine_combine, (unit, zero_rows), True
    )
    depth_step = (
        forward_value + strength * matrix[:, size - 1][None, None, :] * carry_next[:, :, None]
    )
    increment = lax.all_to_all(depth_step, "pencil", split_axis=0, concat_axis=1, tiled=True)
    return density + increment


def solution(mesh):
    in_specs = (P("pencil", None, "slab"), P("pencil", None, "slab"), P(), P(), P(), P())
    out_specs = P("pencil", None, "slab")
    return jax.shard_map(
        per_device, mesh=mesh, in_specs=in_specs, out_specs=out_specs, check_vma=False
    )
```

profile of v0, /device:TPU:0, one launch (start us, length us, event | category | flops | bytes accessed | tf_op | source)
XLA Modules:
  0.0 501.9 jit_solution(8275019180080528345)
XLA Ops:
  0.0 11.2 %fusion.34 = (f32[16,768,1]{2,1,0:T(8,128)}, f32[16,768,1]{2,1,0:T(8,128)}) fusion(f32[16,768,128]{2,1,0:T(8,128)} %param.14), kind=kLoop, calls=%fused_computation.71 | loop fusion | bytes 196608 | tf_op jit(solution)/shard_map/slice | solution.py:13
  11.2 4.4 copy.70
  18.0 4.4 copy.71
  23.7 4.0 copy.41
  27.7 3.9 copy.42
  36.2 5.3 %collective-permute-start.3 = (f32[1,768,130]{1,0,2:T(1,128)S(1)}, f32[1,768,130]{1,0,2:T(1,128)S(1)}, u32[]{:S(2)}, u32[]{:S(2)}) collective-permute-start(f32[1,768,130]{1,0,2:T(1,128)S(1)} %copy.45), channel_id=1, source_target_pairs={{0,1},{1,2},{2,3},{3,4},{4,5},{5,6},{6,7},{8,9},{9,10},{10,11},{11... | collective-permute-start | bytes 1198088 | tf_op jit(solution)/shard_map/ppermute | solution.py:14
  42.2 4.6 collective-permute-done.2
  47.2 10.4 %collective-permute-done.3 = f32[1,768,130]{1,0,2:T(1,128)S(1)} collective-permute-done((f32[1,768,130]{1,0,2:T(1,128)S(1)}, f32[1,768,130]{1,0,2:T(1,128)S(1)}, u32[]{:S(2)}, u32[]{:S(2)}) %collective-permute-start.3) | collective-permute-done | bytes 399392 | tf_op jit(solution)/shard_map/ppermute | solution.py:14
  58.1 30.9 %fusion.17 = f32[16,768,128]{2,1,0:T(8,128)} fusion(f32[16,768,128]{2,1,0:T(8,128)} %param.15, f32[16,768,128]{2,1,0:T(8,128)} %param.14, f32[16,768,1]{2,1,0:T(8,128)} %copy.41, f32[16,768,1]{2,1,0:T(8,128)} %copy.42, f32[1,768,130]{2,1,0:T(8,128)S(1)} %copy.46, f32[1,768,130]{2,1,0:T(8,128)S(1)} %copy.44, f32[]{:T(128)} %bitcast.16, f32[]{:T(128)} %bitcast.15, ...), kind=kLoop, calls=%fused_computation.35 | loop fusion | flops 34603008 | bytes 19771404 | tf_op jit(solution)/shard_map/add | solution.py:81
  89.0 24.1 %while.70 = (s32[]{:T(128)}, f32[16,6,128,128]{3,2,1,0:T(8,128)}, f32[16,128]{1,0:T(8,128)S(1)}, f32[6,128,128]{2,1,0:T(8,128)S(1)}, f32[16,6,128,128]{3,2,1,0:T(8,128)}, /*index=5*/f32[]{:T(128)}, s32[]{:T(128)}) while((s32[]{:T(128)}, f32[16,6,128,128]{3,2,1,0:T(8,128)}, f32[16,128]{1,0:T(8,128)S(1)}, f32[6,128,128]{2,1,0:T(8,128)S(1)}, ...), condition=%wide.region_1.2_spmd, body=%wide.region_0.1_spmd.sunk | while | flops 403177600 | bytes 3370069 | solution.py:52
  113.2 23.1 %while.71 = (s32[]{:T(128)}, f32[16,6,128,128]{3,2,1,0:T(8,128)}, f32[16,128]{1,0:T(8,128)S(1)}, f32[]{:T(128)}, f32[6,128,128]{2,1,0:T(8,128)S(1)}, /*index=5*/s32[]{:T(128)}, s32[]{:T(128)}, s32[]{:T(128)}, s32[]{:T(128)}) while((s32[]{:T(128)}, f32[16,6,128,128]{3,2,1,0:T(8,128)}, f32[16,128]{1,0:T(8,128)S(1)}, f32[]{:T(128)}, ...), condition=%wide.region_3.4_spmd, body=%wide.region_2.3_spmd.sunk | while | flops 528518 | bytes 5555867 | solution.py:63
  136.3 9.0 %copy.52 = f32[16,6,128,128]{3,0,2,1:T(8,128)} copy(f32[16,6,128,128]{3,2,1,0:T(8,128)} %get-tuple-element.414) | data formatting | bytes 12582912 | tf_op jit(solution)/shard_map/while | solution.py:63
  145.3 5.9 %all-to-all-start = ((f32[16,768,128]{2,0,1:T(8,128)}), f32[16,768,128]{2,0,1:T(8,128)}, u32[]{:S(2)}, u32[]{:S(2)}) async-start(f32[16,768,128]{2,0,1:T(8,128)} %bitcast.110), calls=%async_computation | async-start | bytes 12582912 | tf_op jit(solution)/shard_map/all_to_all | solution.py:85
  156.4 7.5 %all-reduce.3 = (f32[4]{0:T(128)S(1)}, f32[4]{0:T(128)S(1)}) all-reduce(f32[4]{0:T(128)S(1)} %dynamic-update-slice, f32[4]{0:T(128)S(1)} %dynamic-update-slice.1), channel_id=1, replica_groups=mesh['slab'=4,'pencil'=8] {'slab'}, use_global_device_ids=true, to_apply=%add.1 | all-reduce | flops 8 | bytes 64
  165.4 124.3 %all-to-all-done = f32[16,768,128]{2,0,1:T(8,128)} async-done(((f32[16,768,128]{2,0,1:T(8,128)}), f32[16,768,128]{2,0,1:T(8,128)}, u32[]{:S(2)}, u32[]{:S(2)}) %all-to-all-start) | async-done | bytes 6291488 | tf_op jit(solution)/shard_map/all_to_all | solution.py:85
  289.7 4.7 copy.54
  294.4 13.4 %fusion.9 = f32[12288,128]{1,0:T(8,128)S(1)} fusion(f32[16,8,96,128]{3,2,1,0:T(8,128)S(1)} %bitcast.107, f32[128]{0:T(128)S(1)} %get-tuple-element.498, f32[128]{0:T(128)S(1)} %get-tuple-element.497, f32[1,128,128]{2,1,0:T(8,128)S(1)} %copy-done.3), kind=kOutput, calls=%fused_computation.26 | convolution fusion | flops 2419064832 | bytes 12649472 | tf_op jit(solution)/shard_map/while/body/eval_jaxpr/pkq,jk->pjq/dot_general | solution.py:46
  307.8 6.4 %fusion.29 = f32[128,96,128]{0,2,1:T(8,128)S(1)} fusion(f32[128,96,128]{0,2,1:T(8,128)S(1)} %bitcast.108, f32[4,128,128]{2,1,0:T(8,128)S(1)} %copy-done, s32[]{:T(128)S(6)} %select_n.60), kind=kOutput, calls=%fused_computation.65 | convolution fusion | flops 2415919104 | bytes 12648452 | tf_op jit(solution)/shard_map/yxk,jk->yxj/dot_general | solution.py:92
  317.0 5.8 %all-gather = f32[512,96,1]{0,2,1:T(1,128)S(1)} all-gather(f32[128,96,1]{0,2,1:T(1,128)S(1)} %slice.140), channel_id=2, replica_groups=mesh['slab'=4,'pencil'=8] {'slab'}, dimensions={0}, use_global_device_ids=true | all-gather | bytes 245760 | tf_op jit(solution)/shard_map/all_gather | solution.py:24
  326.8 10.0 %all-gather.1 = f32[512,96,1]{0,2,1:T(1,128)S(1)} all-gather(f32[128,96,1]{0,2,1:T(1,128)S(1)} %slice.143), channel_id=3, replica_groups=mesh['slab'=4,'pencil'=8] {'slab'}, dimensions={0}, use_global_device_ids=true | all-gather | bytes 245760 | tf_op jit(solution)/shard_map/all_gather | solution.py:24
  336.9 4.3 while.73
  341.3 7.1 %multiply_add_fusion = f32[128,96,128]{0,2,1:T(8,128)} fusion(f32[128,96]{0,1:T(8,128)S(1)} %copy.59, f32[128]{0:T(128)S(1)} %get-tuple-element.495, f32[128,96,128]{0,2,1:T(8,128)} %copy-done.1, f32[128,96]{0,1:T(8,128)S(1)} %copy.57, f32[128]{0:T(128)S(1)} %get-tuple-element.496), kind=kLoop, calls=%fused_computation.50 | loop fusion | flops 6291456 | bytes 12682240 | tf_op jit(solution)/shard_map/add | solution.py:109
  348.4 6.6 %copy.60 = f32[128,96,128]{2,1,0:T(8,128)} copy(f32[128,96,128]{0,2,1:T(8,128)} %multiply_add_fusion) | data formatting | bytes 12582912 | tf_op jit(solution)/shard_map/add | solution.py:109
  355.0 141.7 %all_to_all.33 = f32[128,96,128]{2,1,0:T(8,128)S(1)} all-to-all(f32[128,96,128]{2,1,0:T(8,128)} %copy.60), channel_id=1, replica_groups=mesh['slab'=4,'pencil'=8] {'pencil'}, dimensions={0} | all-to-all | bytes 12582912 | tf_op jit(solution)/shard_map/all_to_all | solution.py:111
  (128 shorter events, 76.8 us)
Async XLA Ops:
  0.0 151.2 %copy-start = (f32[4,128,128]{2,1,0:T(8,128)S(1)}, f32[4,128,128]{2,1,0:T(8,128)}, u32[]{:S(2)}) copy-start(f32[4,128,128]{2,1,0:T(8,128)} %param.19) | copy-start | bytes 786436
  15.6 8.1 %collective-permute-start = (f32[16,768,1]{1,0,2:T(8,128)S(1)}, f32[16,768,1]{1,0,2:T(8,128)S(1)}, u32[]{:S(2)}, u32[]{:S(2)}) collective-permute-start(f32[16,768,1]{1,0,2:T(8,128)S(1)} %copy.70), channel_id=1, source_target_pairs={{0,8},{8,16},{16,24},{1,9},{9,17},{17,25},{2,10},{10,18},{18,26},{... | collective-permute-start | bytes 147464 | tf_op jit(solution)/shard_map/ppermute | solution.py:14
  22.4 5.3 %collective-permute-start.1 = (f32[16,768,1]{1,0,2:T(8,128)S(1)}, f32[16,768,1]{1,0,2:T(8,128)S(1)}, u32[]{:S(2)}, u32[]{:S(2)}) collective-permute-start(f32[16,768,1]{1,0,2:T(8,128)S(1)} %copy.71), channel_id=1, source_target_pairs={{8,0},{16,8},{24,16},{9,1},{17,9},{25,17},{10,2},{18,10},{26,18},{... | collective-permute-start | bytes 147464 | tf_op jit(solution)/shard_map/ppermute | solution.py:15
  31.7 9.8 %copy-start.4 = (f32[3]{0:T(128)S(1)}, f32[3]{0:T(128)}, u32[]{:S(2)}) copy-start(f32[3]{0:T(128)} %param.16) | copy-start | bytes 40
  34.4 12.3 %collective-permute-start.2 = (f32[1,768,130]{1,0,2:T(1,128)S(1)}, f32[1,768,130]{1,0,2:T(1,128)S(1)}, u32[]{:S(2)}, u32[]{:S(2)}) collective-permute-start(f32[1,768,130]{1,0,2:T(1,128)S(1)} %copy.43), channel_id=1, source_target_pairs={{1,0},{2,1},{3,2},{4,3},{5,4},{6,5},{7,6},{9,8},{10,9},{11,10},{12... | collective-permute-start | bytes 1198088 | tf_op jit(solution)/shard_map/ppermute | solution.py:15
  36.2 21.4 %collective-permute-start.3 = (f32[1,768,130]{1,0,2:T(1,128)S(1)}, f32[1,768,130]{1,0,2:T(1,128)S(1)}, u32[]{:S(2)}, u32[]{:S(2)}) collective-permute-start(f32[1,768,130]{1,0,2:T(1,128)S(1)} %copy.45), channel_id=1, source_target_pairs={{0,1},{1,2},{2,3},{3,4},{4,5},{5,6},{6,7},{8,9},{9,10},{10,11},{11... | collective-permute-start | bytes 1198088 | tf_op jit(solution)/shard_map/ppermute | solution.py:14
  58.1 30.9 %copy-start.2 = (f32[6,128,128]{2,1,0:T(8,128)S(1)}, f32[6,128,128]{2,1,0:T(8,128)}, u32[]{:S(2)}) copy-start(f32[6,128,128]{2,1,0:T(8,128)} %param.17) | copy-start | bytes 1179652
  145.3 9.0 %copy-start.5 = (u32[32]{0:T(128)S(1)}, u32[32]{0:T(128)}, u32[]{:S(2)}) copy-start(u32[32]{0:T(128)} %constant.197) | copy-start | bytes 388
  145.3 19.3 %copy-start.3 = (f32[1,128,128]{2,1,0:T(8,128)S(1)}, f32[1,128,128]{2,1,0:T(8,128)}, u32[]{:S(2)}) copy-start(f32[1,128,128]{2,1,0:T(8,128)} %param.18) | copy-start | bytes 196612
  145.3 144.4 %all-to-all-start = ((f32[16,768,128]{2,0,1:T(8,128)}), f32[16,768,128]{2,0,1:T(8,128)}, u32[]{:S(2)}, u32[]{:S(2)}) async-start(f32[16,768,128]{2,0,1:T(8,128)} %bitcast.110), calls=%async_computation | async-start | bytes 12582912 | tf_op jit(solution)/shard_map/all_to_all | solution.py:85
  314.2 2.7 copy-start.1
  355.0 142.4 %slice-start = ((s8[6291456]{0:T(1024)(128)(4,1)}), s8[4194304]{0:T(1024)(128)(4,1)S(1)}, s32[]{:S(2)}) async-start(s8[6291456]{0:T(1024)(128)(4,1)} %bitcast.105), calls=%async_computation.2 | async-start | bytes 8388608
  496.7 1.6 slice-start.1
where the time goes:
time: 507 us; the launch traced here: 502 us
  blocking collectives  165 us (33%)
  waiting for transfers between devices  139 us (27%)
  other arithmetic  73.9 us (15%)
  local copies, waits for them, and re-layouts  64.7 us (13%)
  matrix products  39.3 us (8%)
  starting transfers between devices  16.2 us (3%)
    all_to_all x1, blocking collectives, per_device(): lax.all_to_all(depth_step, 'pencil', split_axis=0, concat_axis=1, tiled=T...  142 us
    all_to_all x1, waiting for transfers between devices, per_device(): lax.all_to_all(width_step, 'pencil', split_axis=1, concat_axis=0, tiled=T...  124 us
    dot_general x7, matrix products, forward(): jnp.einsum('pkq,jk->pjq', piece, matrix, precision=lax.Precision.HIGHEST)  32.9 us
    add x1, other arithmetic, per_device(): 2.0 * (coupling[0] * along_width + coupling[1] * along_height + coupling[...  30.9 us
    all_gather x2, blocking collectives, entering(): gathered = jax.tree.map(lambda a: lax.all_gather(a, axis), part)  15.8 us
    unnamed x23, local copies, waits for them, and re-layouts  14.6 us
    dynamic_slice x6, other arithmetic, backward(): value = lax.dynamic_index_in_dim(result, current, 1, keepdims=False)  14.4 us
    slice x2, local copies, waits for them, and re-layouts, extended(): leading = lax.slice_in_dim(value, 0, width, axis=dim)  11.6 us
  transfers between devices with their start and end apart: 5, of which 3 were waited for; matrix products, arithmetic and copies ran while one was open for 3% of the time, Pallas kernels for 0%

commit v1 on v0

--- a/solution.py
+++ b/solution.py
@@ -2,6 +2,19 @@
 import jax.numpy as jnp
 from jax import lax
 from jax.sharding import PartitionSpec as P
+
+
+def start_the_rails(body, at_axis, patch):
+    v1 = body.shape
+    return jnp.moveaxis(
+        body.reshape(*v1[:at_axis], patch, v1[at_axis] // patch, *v1[at_axis + 1 :]), at_axis, 0
+    )
+
+
+def divide_patch(chunk, axis_k):
+    chunk = jnp.moveaxis(chunk, 0, axis_k)
+    built = chunk.shape
+    return chunk.reshape(*built[:axis_k], built[axis_k] * built[axis_k + 1], *built[axis_k + 2 :])
 
 
 def extended(value, sides, width):
@@ -108,7 +121,17 @@
     depth_step = (
         forward_value + strength * matrix[:, size - 1][None, None, :] * carry_next[:, :, None]
     )
-    increment = lax.all_to_all(depth_step, "pencil", split_axis=0, concat_axis=1, tiled=True)
+    out_arr = lax.axis_size("pencil")
+    shaped, v_next = (out_arr, lax.axis_index("pencil"))
+    placed = start_the_rails(depth_step, 0, shaped)
+    crops = [placed[v_next]]
+    for hop_no in range(1, shaped):
+        row_out = placed[v_next ^ hop_no]
+        y1 = lax.ppermute(row_out, "pencil", [(h, h ^ hop_no) for h in range(shaped)])
+        crops.append(y1)
+    opened = jnp.stack(crops)
+    placed = opened[v_next ^ jnp.arange(shaped)]
+    increment = divide_patch(placed, 1)
     return density + increment
 
 

time: 507 us -> 519 us (1.024)
  the two profiles are of different devices: /device:TPU:0 before, /device:TPU:8 now
where the time goes in v1:
time: 519 us; the launch traced here: 514 us
  waiting for transfers between devices  263 us (51%)
  local copies, waits for them, and re-layouts  84.5 us (16%)
  other arithmetic  74.1 us (14%)
  matrix products  39.3 us (8%)
  starting transfers between devices  25.7 us (5%)
  blocking collectives  23.3 us (4%)
    ppermute x7, waiting for transfers between devices, per_device(): lax.ppermute(row_out, 'pencil', [(h, h ^ hop_no) for h in range(shaped)])  127 us
    all_to_all x1, waiting for transfers between devices, per_device(): lax.all_to_all(width_step, 'pencil', split_axis=1, concat_axis=0, tiled=T...  122 us
    dot_general x7, matrix products, forward(): jnp.einsum('pkq,jk->pjq', piece, matrix, precision=lax.Precision.HIGHEST)  32.9 us
    add x1, other arithmetic, per_device(): 2.0 * (coupling[0] * along_width + coupling[1] * along_height + coupling[...  30.9 us
    unnamed x29, local copies, waits for them, and re-layouts  19.8 us
    all_gather x2, blocking collectives, entering(): gathered = jax.tree.map(lambda a: lax.all_gather(a, axis), part)  16.1 us
    dynamic_slice x6, other arithmetic, backward(): value = lax.dynamic_index_in_dim(result, current, 1, keepdims=False)  14.4 us
    ppermute x2, waiting for transfers between devices, extended(): after = lax.ppermute(leading, axis, down)  13.6 us
  transfers between devices with their start and end apart: 12, of which 9 were waited for; matrix products, arithmetic and copies ran while one was open for 4% of the time, Pallas kernels for 0%

profile of v1, /device:TPU:8, one launch (start us, length us, event | category | flops | bytes accessed | tf_op | source)
XLA Modules:
  0.0 513.6 jit_solution(18121074439105657277)
XLA Ops:
  0.0 11.2 %fusion.35 = (f32[16,768,1]{2,1,0:T(8,128)}, f32[16,768,1]{2,1,0:T(8,128)}) fusion(f32[16,768,128]{2,1,0:T(8,128)} %param.14), kind=kLoop, calls=%fused_computation.90 | loop fusion | bytes 196608 | tf_op jit(solution)/shard_map/slice | solution.py:26
  17.3 4.4 copy.71
  41.3 13.6 %collective-permute-done.2 = f32[1,768,130]{1,0,2:T(1,128)S(1)} collective-permute-done((f32[1,768,130]{1,0,2:T(1,128)S(1)}, f32[1,768,130]{1,0,2:T(1,128)S(1)}, u32[]{:S(2)}, u32[]{:S(2)}) %collective-permute-start.2) | collective-permute-done | bytes 399392 | tf_op jit(solution)/shard_map/ppermute | solution.py:28
  56.6 30.9 %fusion.17 = f32[16,768,128]{2,1,0:T(8,128)} fusion(f32[16,768,128]{2,1,0:T(8,128)} %param.15, f32[16,768,128]{2,1,0:T(8,128)} %param.14, f32[16,768,1]{2,1,0:T(8,128)} %copy.41, f32[16,768,1]{2,1,0:T(8,128)} %copy.42, f32[1,768,130]{2,1,0:T(8,128)S(1)} %copy.46, f32[1,768,130]{2,1,0:T(8,128)S(1)} %copy.44, f32[]{:T(128)} %bitcast.16, f32[]{:T(128)} %bitcast.15, ...), kind=kLoop, calls=%fused_computation.36 | loop fusion | flops 34603008 | bytes 19771404 | tf_op jit(solution)/shard_map/add | solution.py:94
  87.5 24.2 %while.70 = (s32[]{:T(128)}, f32[16,6,128,128]{3,2,1,0:T(8,128)}, f32[16,128]{1,0:T(8,128)S(1)}, f32[6,128,128]{2,1,0:T(8,128)S(1)}, f32[16,6,128,128]{3,2,1,0:T(8,128)}, /*index=5*/f32[]{:T(128)}, s32[]{:T(128)}) while((s32[]{:T(128)}, f32[16,6,128,128]{3,2,1,0:T(8,128)}, f32[16,128]{1,0:T(8,128)S(1)}, f32[6,128,128]{2,1,0:T(8,128)S(1)}, ...), condition=%wide.region_1.2_spmd, body=%wide.region_0.1_spmd.sunk | while | flops 403177600 | bytes 3370069 | solution.py:65
  111.7 23.2 %while.71 = (s32[]{:T(128)}, f32[16,6,128,128]{3,2,1,0:T(8,128)}, f32[16,128]{1,0:T(8,128)S(1)}, f32[]{:T(128)}, f32[6,128,128]{2,1,0:T(8,128)S(1)}, /*index=5*/s32[]{:T(128)}, s32[]{:T(128)}, s32[]{:T(128)}, s32[]{:T(128)}) while((s32[]{:T(128)}, f32[16,6,128,128]{3,2,1,0:T(8,128)}, f32[16,128]{1,0:T(8,128)S(1)}, f32[]{:T(128)}, ...), condition=%wide.region_3.4_spmd, body=%wide.region_2.3_spmd.sunk | while | flops 528518 | bytes 5555867 | solution.py:76
  134.9 9.0 %copy.52 = f32[16,6,128,128]{3,0,2,1:T(8,128)} copy(f32[16,6,128,128]{3,2,1,0:T(8,128)} %get-tuple-element.414) | data formatting | bytes 12582912 | tf_op jit(solution)/shard_map/while | solution.py:76
  143.9 6.4 %all-to-all-start = ((f32[16,768,128]{2,0,1:T(8,128)}), f32[16,768,128]{2,0,1:T(8,128)}, u32[]{:S(2)}, u32[]{:S(2)}) async-start(f32[16,768,128]{2,0,1:T(8,128)} %bitcast.139), calls=%async_computation | async-start | bytes 12582912 | tf_op jit(solution)/shard_map/all_to_all | solution.py:98
  155.4 7.2 %all-reduce.3 = (f32[4]{0:T(128)S(1)}, f32[4]{0:T(128)S(1)}) all-reduce(f32[4]{0:T(128)S(1)} %dynamic-update-slice, f32[4]{0:T(128)S(1)} %dynamic-update-slice.1), channel_id=1, replica_groups=mesh['slab'=4,'pencil'=8] {'slab'}, use_global_device_ids=true, to_apply=%add.1 | all-reduce | flops 8 | bytes 64
  164.2 122.0 %all-to-all-done = f32[16,768,128]{2,0,1:T(8,128)} async-done(((f32[16,768,128]{2,0,1:T(8,128)}), f32[16,768,128]{2,0,1:T(8,128)}, u32[]{:S(2)}, u32[]{:S(2)}) %all-to-all-start) | async-done | bytes 6291488 | tf_op jit(solution)/shard_map/all_to_all | solution.py:98
  286.2 4.7 copy.54
  290.9 13.4 %fusion.9 = f32[12288,128]{1,0:T(8,128)S(1)} fusion(f32[16,8,96,128]{3,2,1,0:T(8,128)S(1)} %bitcast.136, f32[128]{0:T(128)S(1)} %get-tuple-element.498, f32[128]{0:T(128)S(1)} %get-tuple-element.497, f32[1,128,128]{2,1,0:T(8,128)S(1)} %copy-done.3), kind=kOutput, calls=%fused_computation.27 | convolution fusion | flops 2419064832 | bytes 12649472 | tf_op jit(solution)/shard_map/while/body/eval_jaxpr/pkq,jk->pjq/dot_general | solution.py:59
  304.3 6.4 %fusion.29 = f32[128,96,128]{0,2,1:T(8,128)S(1)} fusion(f32[128,96,128]{0,2,1:T(8,128)S(1)} %bitcast.137, f32[4,128,128]{2,1,0:T(8,128)S(1)} %copy-done, s32[]{:T(128)S(6)} %select_n.94), kind=kOutput, calls=%fused_computation.81 | convolution fusion | flops 2415919104 | bytes 12648452 | tf_op jit(solution)/shard_map/yxk,jk->yxj/dot_general | solution.py:105
  313.5 5.8 %all-gather = f32[512,96,1]{0,2,1:T(1,128)S(1)} all-gather(f32[128,96,1]{0,2,1:T(1,128)S(1)} %slice.142), channel_id=2, replica_groups=mesh['slab'=4,'pencil'=8] {'slab'}, dimensions={0}, use_global_device_ids=true | all-gather | bytes 245760 | tf_op jit(solution)/shard_map/all_gather | solution.py:37
  323.3 10.3 %all-gather.1 = f32[512,96,1]{0,2,1:T(1,128)S(1)} all-gather(f32[128,96,1]{0,2,1:T(1,128)S(1)} %slice.145), channel_id=3, replica_groups=mesh['slab'=4,'pencil'=8] {'slab'}, dimensions={0}, use_global_device_ids=true | all-gather | bytes 245760 | tf_op jit(solution)/shard_map/all_gather | solution.py:37
  337.8 7.1 %multiply_add_fusion = f32[128,96,128]{0,2,1:T(8,128)} fusion(f32[128,96]{0,1:T(8,128)S(1)} %copy.59, f32[128]{0:T(128)S(1)} %get-tuple-element.495, f32[128,96,128]{0,2,1:T(8,128)} %copy-done.1, f32[128,96]{0,1:T(8,128)S(1)} %copy.57, f32[128]{0:T(128)S(1)} %get-tuple-element.496), kind=kLoop, calls=%fused_computation.51 | loop fusion | flops 6291456 | bytes 12682240 | tf_op jit(solution)/shard_map/add | solution.py:122
  344.8 7.0 %copy.60 = f32[128,96,128]{2,1,0:T(8,128)} copy(f32[128,96,128]{0,2,1:T(8,128)} %multiply_add_fusion) | data formatting | bytes 12582912 | tf_op jit(solution)/shard_map/add | solution.py:122
  363.9 10.4 %collective-permute-done.4 = f32[16,96,128]{2,1,0:T(8,128)S(1)} collective-permute-done((f32[16,96,128]{2,1,0:T(8,128)S(1)}, f32[16,96,128]{2,1,0:T(8,128)S(1)}, u32[]{:S(2)}, u32[]{:S(2)}) %collective-permute-start.4) | collective-permute-done | bytes 786464 | tf_op jit(solution)/shard_map/ppermute | solution.py:130
  375.9 33.0 %collective-permute-done.5 = f32[16,96,128]{2,1,0:T(8,128)S(1)} collective-permute-done((f32[16,96,128]{2,1,0:T(8,128)S(1)}, f32[16,96,128]{2,1,0:T(8,128)S(1)}, u32[]{:S(2)}, u32[]{:S(2)}) %collective-permute-start.5) | collective-permute-done | bytes 786464 | tf_op jit(solution)/shard_map/ppermute | solution.py:130
  411.2 12.4 %collective-permute-done.6 = f32[16,96,128]{2,1,0:T(8,128)S(1)} collective-permute-done((f32[16,96,128]{2,1,0:T(8,128)S(1)}, f32[16,96,128]{2,1,0:T(8,128)S(1)}, u32[]{:S(2)}, u32[]{:S(2)}) %collective-permute-start.6) | collective-permute-done | bytes 786464 | tf_op jit(solution)/shard_map/ppermute | solution.py:130
  425.4 39.6 %collective-permute-done.8 = f32[16,96,128]{2,1,0:T(8,128)S(1)} collective-permute-done((f32[16,96,128]{2,1,0:T(8,128)S(1)}, f32[16,96,128]{2,1,0:T(8,128)S(1)}, u32[]{:S(2)}, u32[]{:S(2)}) %collective-permute-start.8) | collective-permute-done | bytes 786464 | tf_op jit(solution)/shard_map/ppermute | solution.py:130
  466.0 17.0 %collective-permute-done.9 = f32[16,96,128]{2,1,0:T(8,128)S(1)} collective-permute-done((f32[16,96,128]{2,1,0:T(8,128)S(1)}, f32[16,96,128]{2,1,0:T(8,128)S(1)}, u32[]{:S(2)}, u32[]{:S(2)}) %collective-permute-start.9) | collective-permute-done | bytes 786464 | tf_op jit(solution)/shard_map/ppermute | solution.py:130
  483.9 14.1 %collective-permute-done.10 = f32[16,96,128]{2,1,0:T(8,128)S(1)} collective-permute-done((f32[16,96,128]{2,1,0:T(8,128)S(1)}, f32[16,96,128]{2,1,0:T(8,128)S(1)}, u32[]{:S(2)}, u32[]{:S(2)}) %collective-permute-start.10) | collective-permute-done | bytes 786464 | tf_op jit(solution)/shard_map/ppermute | solution.py:130
  499.0 6.6 %gather_fusion = f32[8,16,96,128]{3,2,1,0:T(8,128)} fusion(f32[8,16,96,128]{3,2,1,0:T(8,128)} %bitcast_dynamic-update-slice_fusion.1, s32[1024]{0:T(1024)S(1)} %pad_clamp_fusion), kind=kCustom, calls=%fused_computation | custom fusion | bytes 12582944 | tf_op jit(solution)/shard_map/gather | solution.py:133
  (152 shorter events, 121.7 us)
Async XLA Ops:
  0.0 150.3 %copy-start = (f32[4,128,128]{2,1,0:T(8,128)S(1)}, f32[4,128,128]{2,1,0:T(8,128)}, u32[]{:S(2)}) copy-start(f32[4,128,128]{2,1,0:T(8,128)} %param.19) | copy-start | bytes 786436
  15.6 7.5 %collective-permute-start = (f32[16,768,1]{1,0,2:T(8,128)S(1)}, f32[16,768,1]{1,0,2:T(8,128)S(1)}, u32[]{:S(2)}, u32[]{:S(2)}) collective-permute-start(f32[16,768,1]{1,0,2:T(8,128)S(1)} %copy.70), channel_id=1, source_target_pairs={{0,8},{8,16},{16,24},{1,9},{9,17},{17,25},{2,10},{10,18},{18,26},{... | collective-permute-start | bytes 147464 | tf_op jit(solution)/shard_map/ppermute | solution.py:27
  21.8 5.3 %collective-permute-start.1 = (f32[16,768,1]{1,0,2:T(8,128)S(1)}, f32[16,768,1]{1,0,2:T(8,128)S(1)}, u32[]{:S(2)}, u32[]{:S(2)}) collective-permute-start(f32[16,768,1]{1,0,2:T(8,128)S(1)} %copy.71), channel_id=1, source_target_pairs={{8,0},{16,8},{24,16},{9,1},{17,9},{25,17},{10,2},{18,10},{26,18},{... | collective-permute-start | bytes 147464 | tf_op jit(solution)/shard_map/ppermute | solution.py:28
  31.0 9.6 %copy-start.4 = (f32[3]{0:T(128)S(1)}, f32[3]{0:T(128)}, u32[]{:S(2)}) copy-start(f32[3]{0:T(128)} %param.16) | copy-start | bytes 40
  33.7 21.1 %collective-permute-start.2 = (f32[1,768,130]{1,0,2:T(1,128)S(1)}, f32[1,768,130]{1,0,2:T(1,128)S(1)}, u32[]{:S(2)}, u32[]{:S(2)}) collective-permute-start(f32[1,768,130]{1,0,2:T(1,128)S(1)} %copy.43), channel_id=1, source_target_pairs={{1,0},{2,1},{3,2},{4,3},{5,4},{6,5},{7,6},{9,8},{10,9},{11,10},{12... | collective-permute-start | bytes 1198088 | tf_op jit(solution)/shard_map/ppermute | solution.py:28
  37.5 18.6 %collective-permute-start.3 = (f32[1,768,130]{1,0,2:T(1,128)S(1)}, f32[1,768,130]{1,0,2:T(1,128)S(1)}, u32[]{:S(2)}, u32[]{:S(2)}) collective-permute-start(f32[1,768,130]{1,0,2:T(1,128)S(1)} %copy.45), channel_id=1, source_target_pairs={{0,1},{1,2},{2,3},{3,4},{4,5},{5,6},{6,7},{8,9},{9,10},{10,11},{11... | collective-permute-start | bytes 1198088 | tf_op jit(solution)/shard_map/ppermute | solution.py:27
  56.6 30.9 %copy-start.2 = (f32[6,128,128]{2,1,0:T(8,128)S(1)}, f32[6,128,128]{2,1,0:T(8,128)}, u32[]{:S(2)}) copy-start(f32[6,128,128]{2,1,0:T(8,128)} %param.17) | copy-start | bytes 1179652
  143.9 9.4 %copy-start.5 = (u32[32]{0:T(128)S(1)}, u32[32]{0:T(128)}, u32[]{:S(2)}) copy-start(u32[32]{0:T(128)} %constant.215) | copy-start | bytes 388
  143.9 19.4 %copy-start.3 = (f32[1,128,128]{2,1,0:T(8,128)S(1)}, f32[1,128,128]{2,1,0:T(8,128)}, u32[]{:S(2)}) copy-start(f32[1,128,128]{2,1,0:T(8,128)} %param.18) | copy-start | bytes 196612
  143.9 142.3 %all-to-all-start = ((f32[16,768,128]{2,0,1:T(8,128)}), f32[16,768,128]{2,0,1:T(8,128)}, u32[]{:S(2)}, u32[]{:S(2)}) async-start(f32[16,768,128]{2,0,1:T(8,128)} %bitcast.139), calls=%async_computation | async-start | bytes 12582912 | tf_op jit(solution)/shard_map/all_to_all | solution.py:98
  310.7 2.7 copy-start.1
  355.9 18.4 %collective-permute-start.4 = (f32[16,96,128]{2,1,0:T(8,128)S(1)}, f32[16,96,128]{2,1,0:T(8,128)S(1)}, u32[]{:S(2)}, u32[]{:S(2)}) collective-permute-start(f32[16,96,128]{2,1,0:T(8,128)S(1)} %get-tuple-element.555), channel_id=1, source_target_pairs={{0,1},{1,0},{2,3},{3,2},{4,5},{5,4},{6,7},{7,6},{8,9},{9,8},{10,11... | collective-permute-start | bytes 2359304 | tf_op jit(solution)/shard_map/ppermute | solution.py:130
  356.6 52.4 %collective-permute-start.5 = (f32[16,96,128]{2,1,0:T(8,128)S(1)}, f32[16,96,128]{2,1,0:T(8,128)S(1)}, u32[]{:S(2)}, u32[]{:S(2)}) collective-permute-start(f32[16,96,128]{2,1,0:T(8,128)S(1)} %get-tuple-element.554), channel_id=1, source_target_pairs={{0,2},{1,3},{2,0},{3,1},{4,6},{5,7},{6,4},{7,5},{8,10},{9,11},{10,... | collective-permute-start | bytes 2359304 | tf_op jit(solution)/shard_map/ppermute | solution.py:130
  360.0 63.5 %collective-permute-start.6 = (f32[16,96,128]{2,1,0:T(8,128)S(1)}, f32[16,96,128]{2,1,0:T(8,128)S(1)}, u32[]{:S(2)}, u32[]{:S(2)}) collective-permute-start(f32[16,96,128]{2,1,0:T(8,128)S(1)} %get-tuple-element.553), channel_id=1, source_target_pairs={{0,3},{1,2},{2,1},{3,0},{4,7},{5,6},{6,5},{7,4},{8,11},{9,10},{10,... | collective-permute-start | bytes 2359304 | tf_op jit(solution)/shard_map/ppermute | solution.py:130
  360.1 64.4 %collective-permute-start.7 = (f32[16,96,128]{2,1,0:T(8,128)S(1)}, f32[16,96,128]{2,1,0:T(8,128)S(1)}, u32[]{:S(2)}, u32[]{:S(2)}) collective-permute-start(f32[16,96,128]{2,1,0:T(8,128)S(1)} %get-tuple-element.552), channel_id=1, source_target_pairs={{0,4},{1,5},{2,6},{3,7},{4,0},{5,1},{6,2},{7,3},{8,12},{9,13},{10,... | collective-permute-start | bytes 2359304 | tf_op jit(solution)/shard_map/ppermute | solution.py:130
  362.9 102.2 %collective-permute-start.8 = (f32[16,96,128]{2,1,0:T(8,128)S(1)}, f32[16,96,128]{2,1,0:T(8,128)S(1)}, u32[]{:S(2)}, u32[]{:S(2)}) collective-permute-start(f32[16,96,128]{2,1,0:T(8,128)S(1)} %get-tuple-element.551), channel_id=1, source_target_pairs={{0,5},{1,4},{2,7},{3,6},{4,1},{5,0},{6,3},{7,2},{8,13},{9,12},{10,... | collective-permute-start | bytes 2359304 | tf_op jit(solution)/shard_map/ppermute | solution.py:130
  374.3 108.7 %collective-permute-start.9 = (f32[16,96,128]{2,1,0:T(8,128)S(1)}, f32[16,96,128]{2,1,0:T(8,128)S(1)}, u32[]{:S(2)}, u32[]{:S(2)}) collective-permute-start(f32[16,96,128]{2,1,0:T(8,128)S(1)} %get-tuple-element.550), channel_id=1, source_target_pairs={{0,6},{1,7},{2,4},{3,5},{4,2},{5,3},{6,0},{7,1},{8,14},{9,15},{10,... | collective-permute-start | bytes 2359304 | tf_op jit(solution)/shard_map/ppermute | solution.py:130
  408.9 89.1 %collective-permute-start.10 = (f32[16,96,128]{2,1,0:T(8,128)S(1)}, f32[16,96,128]{2,1,0:T(8,128)S(1)}, u32[]{:S(2)}, u32[]{:S(2)}) collective-permute-start(f32[16,96,128]{2,1,0:T(8,128)S(1)} %get-tuple-element.549), channel_id=1, source_target_pairs={{0,7},{1,6},{2,5},{3,4},{4,3},{5,2},{6,1},{7,0},{8,15},{9,14},{10,... | collective-permute-start | bytes 2359304 | tf_op jit(solution)/shard_map/ppermute | solution.py:130
  499.0 10.0 %slice-start = ((s8[6291456]{0:T(1024)(128)(4,1)}), s8[2097152]{0:T(1024)(128)(4,1)S(1)}, s32[]{:S(2)}) async-start(s8[6291456]{0:T(1024)(128)(4,1)} %bitcast.134), calls=%async_computation.1 | async-start | bytes 4194304
  505.6 4.0 slice-start.1
